TPU v7x, 128 devices: a whole 4x4x4 slice. The times are simulated.
128 devices in a mesh: seq: 16 (over y, x_hi, core), head: 8 (over z, x_lo).
Axes of the slice: x: 4 (x_hi: 2, x_lo: 2; x = x_hi * 2 + x_lo), y: 4, z: 4, core: 2. Of those that a mesh axis runs over, the one named last changes fastest.
Arguments:
- d_bytes: bfloat16 [4096, 8192], P('seq', 'head'), may hold values from -6 to 6
- owner_groups: int32 [16, 16], replicated, may hold values from 0 to 255, as said below
- block_order: int32 [16], replicated, may hold values from 0 to 15, each once
- y_in: bfloat16 [4096, 4096], P('seq'), may hold values from -0.29882812 to 0.29882812
- w_proj: bfloat16 [4096, 8192], P('seq', 'head'), may hold values from -0.0625 to 0.0625
- w_out: bfloat16 [2048, 4096], P('head', 'seq'), may hold values from -0.125 to 0.125
- queries: bfloat16 [4096, 2048], P('seq', 'head'), may hold values from -24 to 24
- keys: bfloat16 [4096, 2048], P('seq', 'head'), may hold values from -24 to 24
- values: bfloat16 [4096, 2048], P('seq', 'head'), may hold values from -6 to 6
- attn_out: bfloat16 [4096, 2048], P('seq', 'head'), may hold values from -0.59765625 to 0.59765625
Outputs:
- layer_grad: bfloat16 [4096, 4096], P('seq', 'head')
- grad_proj: bfloat16 [4096, 8192], P('seq', 'head')
- grad_out: bfloat16 [2048, 4096], P('head', 'seq')
- grad_queries: bfloat16 [4096, 2048], P('seq', 'head')
- grad_keys: bfloat16 [4096, 2048], P('seq', 'head')
- grad_values: bfloat16 [4096, 2048], P('seq', 'head')
Inputs may be any that keep to these rules, and one draw needn't show every extreme that they name: `owner_groups`: row o lists the patch groups held by owner o; it holds exactly one group of every seq shard (group g covers patches g * 16 to g * 16 + 15, shard g // 16), and every group appears once. `block_order`: A permutation.
All inputs are finite; a program needn't handle non-finite values.
Results may differ from a plain program's by a relative error of at most 0.03.
Values may be sent and summed in bfloat16 or wider, within the bound.
No kernel may reach another device: no remote copies, remote signals or barrier semaphores. Data moves between devices by JAX's collectives and lax.ppermute only.
A program may use at most 128 MiB of HBM per device.

v0:
```python
import math

import jax
import jax.numpy as jnp
from jax import lax
from jax.sharding import PartitionSpec as P

HEAD_DIM = 128


def in_blocks(shard, dim, peers):
    before, after = (shard.shape[:dim], shard.shape[dim + 1 :])
    return jnp.moveaxis(shard.reshape(*before, peers, -1, *after), dim, 0)


def summed_on_arrival(shard, axis, dim):
    pieces = in_blocks(shard, dim, lax.axis_size(axis))
    arrived = lax.all_to_all(pieces, axis, split_axis=0, concat_axis=0, tiled=True)
    return arrived.astype(jnp.float32).sum(axis=0)


def in_order(pieces, dim):
    shape = list(pieces.shape[1:])
    shape[dim] *= pieces.shape[0]
    return jnp.moveaxis(pieces, 0, dim).reshape(shape)


def from_everyone(shard, axis):
    peers = lax.axis_size(axis)
    return lax.all_to_all(
        jnp.broadcast_to(shard[None], (peers, *shard.shape)), axis, 0, 0, tiled=True
    )


def gathered_copies(shard, axis, dim):
    return in_order(from_everyone(shard, axis), dim)


def in_one_piece(arrays, axis, dim, along):
    both = jnp.concatenate(arrays, axis=along)
    filled, at, gathered = (lax.all_gather(both, axis, axis=dim, tiled=True), 0, [])
    for a in arrays:
        gathered.append(lax.slice_in_dim(filled, at, at + a.shape[along], axis=along))
        at += a.shape[along]
    return tuple(gathered)


def sent_together(arrays, axis, dim, along):
    ends, at = ([], 0)
    for a in arrays[:-1]:
        at += a.shape[along]
        ends.append(at)
    both = jnp.concatenate(arrays, axis=along)
    return tuple(
        jnp.split(lax.psum_scatter(both, axis, scatter_dimension=dim, tiled=True), ends, axis=along)
    )


def body(d_bytes, owner_groups, block_order, y_in, w_proj, w_out, queries, keys, values, attn_out):
    flt = jnp.float32
    half = jnp.bfloat16
    owners = lax.axis_size("seq")
    seq_index = lax.axis_index("seq")
    patch_dev = y_in.shape[0]
    group_rows = patch_dev // owners
    columns = d_bytes.shape[1]
    owner_ids = jnp.arange(owners, dtype=jnp.int32)
    mine = jnp.sum(jnp.where(owner_ids[:, None] == seq_index, owner_groups, 0), axis=0)
    sending = jnp.argsort(mine // owners)
    outgoing = jnp.take(d_bytes.reshape(owners, group_rows, columns), sending, axis=0)
    incoming = lax.all_to_all(outgoing, "seq", split_axis=0, concat_axis=0, tiled=True)
    landing = jnp.sum(
        jnp.where(owner_groups // owners == seq_index, owner_groups % owners, 0), axis=1
    )
    arrival = jnp.argsort(landing)
    natural = jnp.take(incoming, arrival, axis=0).reshape(patch_dev, columns)
    grad_proj = (
        lax.psum_scatter(
            lax.dot_general(
                y_in, natural, (((0,), (0,)), ((), ())), preferred_element_type=flt
            ).astype(jnp.bfloat16),
            "seq",
            scatter_dimension=0,
            tiled=True,
        )
        .astype(jnp.float32)
        .astype(half)
    )
    head_part = lax.dot_general(
        natural,
        lax.all_gather(w_proj, "seq", axis=0, tiled=True),
        (((1,), (1,)), ((), ())),
        preferred_element_type=flt,
    )
    layer_grad = summed_on_arrival(head_part.astype(jnp.bfloat16), "head", 1).astype(half)
    full_grad = gathered_copies(layer_grad, "head", 1)
    width_dev = queries.shape[1]
    attn_grad = lax.dot_general(
        full_grad,
        lax.all_gather(w_out, "seq", axis=1, tiled=True),
        (((1,), (1,)), ((), ())),
        preferred_element_type=flt,
    ).astype(half)
    out_term = lax.dot_general(
        attn_out, full_grad, (((0,), (0,)), ((), ())), preferred_element_type=flt
    )
    grad_out = summed_on_arrival(out_term.astype(jnp.bfloat16), "seq", 1).astype(half)
    heads_dev = width_dev // HEAD_DIM
    scale = 1.0 / math.sqrt(HEAD_DIM)
    query_heads = queries.reshape(patch_dev, heads_dev, HEAD_DIM)
    grad_heads = attn_grad.reshape(patch_dev, heads_dev, HEAD_DIM)
    delta = jnp.sum(
        grad_heads.astype(flt) * attn_out.reshape(patch_dev, heads_dev, HEAD_DIM).astype(flt),
        axis=2,
    ).T
    local_rows = jnp.arange(patch_dev, dtype=jnp.int32)
    my_block = jnp.sum(jnp.where(owner_ids == seq_index, block_order, 0))
    query_pos = my_block * patch_dev + local_rows
    keys_all, values_all = in_one_piece((keys, values), "seq", 0, 1)
    all_rows = keys_all.shape[0]
    block_rows = math.gcd(512, all_rows)
    block_count = all_rows // block_rows
    row_ids = jnp.arange(all_rows, dtype=jnp.int32)
    row_owner = row_ids // patch_dev
    key_pos = (
        jnp.sum(
            jnp.where(row_owner[:, None] == owner_ids[None, :], block_order[None, :], 0), axis=1
        )
        * patch_dev
        + row_ids % patch_dev
    )
    key_blocks = keys_all.reshape(block_count, block_rows, heads_dev, HEAD_DIM)
    value_blocks = values_all.reshape(block_count, block_rows, heads_dev, HEAD_DIM)
    pos_blocks = key_pos.reshape(block_count, block_rows)

    def scores_of(key_block, pos_block):
        scores = (
            jnp.einsum("qhd,khd->hqk", query_heads, key_block, preferred_element_type=flt) * scale
        )
        allowed = pos_block[None, :] <= query_pos[:, None]
        return (scores, allowed)

    def statistics(running, pieces):
        highest, totals = running
        key_block, pos_block = pieces
        scores, allowed = scores_of(key_block, pos_block)
        scores = jnp.where(allowed[None], scores, -1e30)
        new_high = jnp.maximum(highest, jnp.max(scores, axis=2))
        weights = jnp.where(allowed[None], jnp.exp(scores - new_high[:, :, None]), 0.0)
        totals = totals * jnp.exp(highest - new_high) + jnp.sum(weights, axis=2)
        return ((new_high, totals), None)

    start_stats = (
        jnp.full((heads_dev, patch_dev), -1e30, flt),
        jnp.zeros((heads_dev, patch_dev), flt),
    )
    (highest, totals), _ = lax.scan(statistics, start_stats, (key_blocks, pos_blocks))
    log_total = highest + jnp.log(totals)

    def backward(grad_query, pieces):
        key_block, value_block, pos_block = pieces
        scores, allowed = scores_of(key_block, pos_block)
        weights = jnp.where(allowed[None], jnp.exp(scores - log_total[:, :, None]), 0.0)
        grad_weights = jnp.einsum(
            "qhd,khd->hqk", grad_heads, value_block, preferred_element_type=flt
        )
        grad_scores = (weights * (grad_weights - delta[:, :, None]) * scale).astype(half)
        weights_low = weights.astype(half)
        grad_query = grad_query + jnp.einsum(
            "hqk,khd->qhd", grad_scores, key_block, preferred_element_type=flt
        )
        key_term = jnp.einsum("hqk,qhd->khd", grad_scores, query_heads, preferred_element_type=flt)
        value_term = jnp.einsum("hqk,qhd->khd", weights_low, grad_heads, preferred_element_type=flt)
        return (grad_query, (key_term, value_term))

    start_grad = jnp.zeros((patch_dev, heads_dev, HEAD_DIM), flt)
    grad_query, (key_terms, value_terms) = lax.scan(
        backward, start_grad, (key_blocks, value_blocks, pos_blocks)
    )
    key_terms = key_terms.reshape(all_rows, width_dev)
    value_terms = value_terms.reshape(all_rows, width_dev)
    grad_keys, grad_values = tuple(
        (
            part.astype(jnp.float32)
            for part in sent_together(
                (key_terms.astype(jnp.bfloat16), value_terms.astype(jnp.bfloat16)), "seq", 0, 1
            )
        )
    )
    grad_queries = grad_query.reshape(patch_dev, width_dev).astype(half)
    return (
        layer_grad,
        grad_proj,
        grad_out,
        grad_queries,
        grad_keys.astype(half),
        grad_values.astype(half),
    )


def solution(mesh):
    placed = (
        P("seq", "head"),
        P(),
        P(),
        P("seq", None),
        P("seq", "head"),
        P("head", "seq"),
        P("seq", "head"),
        P("seq", "head"),
        P("seq", "head"),
        P("seq", "head"),
    )
    return jax.shard_map(
        body,
        mesh=mesh,
        in_specs=placed,
        out_specs=(
            P("seq", "head"),
            P("seq", "head"),
            P("head", "seq"),
            P("seq", "head"),
            P("seq", "head"),
            P("seq", "head"),
        ),
        check_vma=False,
    )
```

profile of v0, /device:TPU:0, one launch (start us, length us, event | category | flops | bytes accessed | tf_op | source)
XLA Modules:
  0.0 408.7 jit_solution(1989037170501856111)
XLA Ops:
  8.0 1.7 pad_maximum_fusion.1
  11.4 1.2 sort.31
  12.6 1.6 gather_fusion
  15.2 7.1 %all-to-all-start = ((bf16[16,16,1024]{2,1,0:T(8,128)(2,1)}), bf16[16,16,1024]{2,1,0:T(8,128)(2,1)S(1)}, u32[]{:S(2)}, u32[]{:S(2)}) async-start(bf16[16,16,1024]{2,1,0:T(8,128)(2,1)} %broadcast_select_fusion.2), calls=%async_computation | async-start | bytes 1048576 | tf_op jit(solution)/shard_map/all_to_all | solution.py:71
  22.3 1.2 sort.32
  23.8 16.4 %all-to-all-done = bf16[16,16,1024]{2,1,0:T(8,128)(2,1)S(1)} async-done(((bf16[16,16,1024]{2,1,0:T(8,128)(2,1)}), bf16[16,16,1024]{2,1,0:T(8,128)(2,1)S(1)}, u32[]{:S(2)}, u32[]{:S(2)}) %all-to-all-start) | async-done | bytes 524320 | tf_op jit(solution)/shard_map/all_to_all | solution.py:71
  40.9 49.9 %all-gather.4.cloned.1.call-done = bf16[4096,1024]{1,0:T(8,128)(2,1)} async-done(((bf16[256,1024]{1,0:T(8,128)(2,1)}), bf16[4096,1024]{1,0:T(8,128)(2,1)}) %all-gather.4.cloned.1.call-update) | async-done | bytes 8388624 | tf_op jit(solution)/shard_map/all_gather | solution.py:91
  90.8 5.8 %convolution_convert_fusion = bf16[256,4096]{1,0:T(8,128)(2,1)S(1)} fusion(bf16[256,1024]{1,0:T(8,128)(2,1)S(1)} %bitcast.139, bf16[4096,1024]{1,0:T(8,128)(2,1)} %all-gather.4.cloned.1.call-done), kind=kOutput, calls=%fused_computation.47 | convolution fusion | flops 2148532224 | bytes 11010048 | tf_op jit(solution)/shard_map/dot_general | solution.py:89
  96.6 1.5 copy.97
  98.1 4.6 %all-to-all-start.1 = ((bf16[8,256,512]{2,1,0:T(8,128)(2,1)}), bf16[8,256,512]{2,1,0:T(8,128)(2,1)}, u32[]{:S(2)}, u32[]{:S(2)}) async-start(bf16[8,256,512]{2,1,0:T(8,128)(2,1)} %bitcast.135), calls=%async_computation.1 | async-start | bytes 4194304 | tf_op jit(solution)/shard_map/all_to_all | solution.py:18
  105.7 5.6 %convert_bitcast_fusion = bf16[4096,1024]{0,1:T(8,128)(2,1)} fusion(bf16[256,1024]{1,0:T(8,128)(2,1)S(1)} %bitcast.140, bf16[256,4096]{1,0:T(8,128)(2,1)S(1)} %copy-done), kind=kOutput, calls=%fused_computation.46 | convolution fusion | flops 2151677952 | bytes 11010048 | tf_op jit(solution)/shard_map/dot_general | solution.py:79
  111.3 38.1 %all-gather.6.cloned.1.call-done = bf16[4096,512]{1,0:T(8,128)(2,1)} async-done(((bf16[256,512]{1,0:T(8,128)(2,1)}), bf16[4096,512]{1,0:T(8,128)(2,1)}) %all-gather.6.cloned.1.call-update) | async-done | bytes 4194320 | tf_op jit(solution)/shard_map/all_gather | solution.py:41
  149.4 4.5 %fusion.40 = (bf16[4096,256]{1,0:T(8,128)(2,1)}, bf16[4096,256]{1,0:T(8,128)(2,1)}) fusion(bf16[4096,512]{1,0:T(8,128)(2,1)} %all-gather.6.cloned.1.call-done), kind=kLoop, calls=%fused_computation.99 | loop fusion | bytes 8388608 | tf_op jit(solution)/shard_map/slice | solution.py:43
  154.0 2.5 reshape.169
  156.5 1.8 copy.70
  158.3 2.0 reduce_sum.80
  160.4 1.5 broadcast_in_dim.101
  161.9 4.8 %all-to-all-start.2 = ((bf16[8,256,512]{1,2,0:T(8,128)(2,1)}), bf16[8,256,512]{1,2,0:T(8,128)(2,1)S(1)}, u32[]{:S(2)}, u32[]{:S(2)}) async-start(bf16[8,256,512]{1,2,0:T(8,128)(2,1)} %broadcast_in_dim.101), calls=%async_computation.3 | async-start | bytes 4194304 | tf_op jit(solution)/shard_map/all_to_all | solution.py:30
  167.0 19.6 %while.28 = (s32[]{:T(128)}, f32[2,256]{1,0:T(2,128)S(1)}, f32[2,256]{1,0:T(2,128)S(1)}, s32[8,512]{1,0:T(8,128)}, bf16[8,512,2,128]{3,1,2,0:T(8,128)(2,1)}, /*i...) while((s32[]{:T(128)}, f32[2,256]{1,0:T(2,128)S(1)}, ...), condition=%wide.region_12.14_spmd.clone, body=%wide.region_9.13_spmd.clone.sunk | while | flops 68815616 | bytes 2918524 | solution.py:157
  167.9 1.3 fusion.76
  170.3 1.3 fusion.76
  172.8 1.3 fusion.76
  175.3 1.3 fusion.76
  177.7 1.3 fusion.76
  180.2 1.3 fusion.76
  182.6 1.3 fusion.76
  185.1 1.3 fusion.76
  186.6 4.1 reshape.170
  190.7 12.7 %all-gather.8.cloned.1.call-done = bf16[256,4096]{1,0:T(8,128)(2,1)} async-done(((bf16[256,256]{1,0:T(8,128)(2,1)}), bf16[256,4096]{1,0:T(8,128)(2,1)}) %all-gather.8.cloned.1.call-update) | async-done | bytes 2097168 | tf_op jit(solution)/shard_map/all_gather | solution.py:100
  203.4 3.1 multiply_reduce_fusion
  206.6 55.9 %while.29 = (s32[]{:T(128)}, f32[256,2,128]{0,2,1:T(8,128)S(1)}, bf16[8,512,2,128]{3,1,2,0:T(8,128)(2,1)}, bf16[8,512,2,128]{3,1,2,0:T(8,128)(2,1)}, bf16[8,512,...) while((s32[]{:T(128)}, f32[256,2,128]{0,2,1:T(8,128)S(1)}, ...), condition=%wide.region_15.17_spmd.clone, body=%wide.region_14.16_spmd.clone.sunk | while | flops 337903872 | bytes 8401075 | solution.py:177
  207.5 1.3 fusion.88
  208.8 1.1 constant_dynamic-slice_fusion.8
  210.3 1.3 fusion.90
  214.5 1.3 fusion.88
  215.8 1.2 constant_dynamic-slice_fusion.8
  217.3 1.3 fusion.90
  221.5 1.3 fusion.88
  222.8 1.2 constant_dynamic-slice_fusion.8
  224.3 1.3 fusion.90
  228.5 1.4 fusion.88
  229.9 1.1 constant_dynamic-slice_fusion.8
  231.4 1.3 fusion.90
  235.5 1.3 fusion.88
  238.3 1.3 fusion.90
  242.5 1.3 fusion.88
  245.3 1.3 fusion.90
  249.5 1.3 fusion.88
  250.8 1.1 constant_dynamic-slice_fusion.8
  252.2 1.3 fusion.90
  256.4 1.3 fusion.88
  257.7 1.2 constant_dynamic-slice_fusion.8
  259.2 1.3 fusion.90
  262.5 3.9 copy.76
  266.4 2.2 copy.75
  269.4 2.3 pad_maximum_fusion
  271.8 1.6 copy-done.3
  273.3 2.0 convolution_convert_fusion.1
  275.4 4.5 %all-to-all-start.3 = ((bf16[16,256,256]{1,2,0:T(8,128)(2,1)}), bf16[16,256,256]{1,2,0:T(8,128)(2,1)}, u32[]{:S(2)}, u32[]{:S(2)}) async-start(bf16[16,256,256]{1,2,0:T(8,128)(2,1)} %bitcast.134), calls=%async_computation.4 | async-start | bytes 4194304 | tf_op jit(solution)/shard_map/all_to_all | solution.py:18
  279.8 37.9 %reduce-scatter.3.cloned.1.call-done = bf16[256,1024]{0,1:T(8,128)(2,1)} async-done(((bf16[4096,1024]{0,1:T(8,128)(2,1)}), bf16[256,1024]{0,1:T(8,128)(2,1)}) %reduce-scatter.3.cloned.1.call-update) | async-done | bytes 524304 | tf_op jit(solution)/shard_map/reduce_scatter | solution.py:78
  317.7 2.2 copy.77
  320.6 1.9 reduce_sum.81
  323.3 77.2 %reduce-scatter.5.cloned.1.call-done = bf16[256,512]{1,0:T(8,128)(2,1)} async-done(((bf16[4096,512]{1,0:T(8,128)(2,1)}), bf16[256,512]{1,0:T(8,128)(2,1)}) %reduce-scatter.5.cloned.1.call-update) | async-done | bytes 262160 | tf_op jit(solution)/shard_map/reduce_scatter | solution.py:55
  400.5 1.7 fusion.41
  (179 shorter events, 46.3 us)
Async XLA Ops:
  7.2 98.5 %copy-start = (bf16[256,4096]{1,0:T(8,128)(2,1)S(1)}, bf16[256,4096]{1,0:T(8,128)(2,1)}, u32[]{:S(2)}) copy-start(bf16[256,4096]{1,0:T(8,128)(2,1)} %param.19) | copy-start | bytes 6291460
  7.2 83.6 %all-gather.4.cloned.1.call-start = ((), (), s32[]{:S(2)}) async-start(), calls=%async_computation.6 | async-start | bytes 8912896 | tf_op jit(solution)/shard_map/all_gather | solution.py:91
  7.9 15.7 %copy-start.12 = (s32[16]{0:T(128)S(1)}, s32[16]{0:T(128)}, u32[]{:S(2)}) copy-start(s32[16]{0:T(128)} %param.18) | copy-start | bytes 196
  7.9 141.5 %all-gather.6.cloned.1.call-start = ((), (), s32[]{:S(2)}) async-start(), calls=%async_computation.8 | async-start | bytes 4456448 | tf_op jit(solution)/shard_map/all_gather | solution.py:41
  9.7 193.7 %all-gather.8.cloned.1.call-start = ((), (), s32[]{:S(2)}) async-start(), calls=%async_computation.9 | async-start | bytes 2228224 | tf_op jit(solution)/shard_map/all_gather | solution.py:100
  15.2 25.0 %all-to-all-start = ((bf16[16,16,1024]{2,1,0:T(8,128)(2,1)}), bf16[16,16,1024]{2,1,0:T(8,128)(2,1)S(1)}, u32[]{:S(2)}, u32[]{:S(2)}) async-start(bf16[16,16,1024]{2,1,0:T(8,128)(2,1)} %broadcast_select_fusion.2), calls=%async_computation | async-start | bytes 1048576 | tf_op jit(solution)/shard_map/all_to_all | solution.py:71
  40.9 55.7 %copy-start.6 = (bf16[16,16,1024]{2,1,0:T(8,128)(2,1)}, bf16[16,16,1024]{2,1,0:T(8,128)(2,1)S(1)}, u32[]{:S(2)}) copy-start(bf16[16,16,1024]{2,1,0:T(8,128)(2,1)S(1)} %broadcast_select_fusion.1) | copy-start | bytes 1572868
  98.1 5.3 %copy-start.11 = (bf16[256,256]{1,0:T(8,128)(2,1)S(1)}, bf16[256,256]{1,0:T(8,128)(2,1)}, u32[]{:S(2)}) copy-start(bf16[256,256]{1,0:T(8,128)(2,1)} %param.22) | copy-start | bytes 393220
  98.1 5.5 %copy-start.10 = (bf16[256,256]{1,0:T(8,128)(2,1)S(1)}, bf16[256,256]{1,0:T(8,128)(2,1)}, u32[]{:S(2)}) copy-start(bf16[256,256]{1,0:T(8,128)(2,1)} %param.25) | copy-start | bytes 393220
  98.1 7.6 %copy-start.7 = (bf16[16,16,1024]{2,1,0:T(8,128)(2,1)S(1)}, bf16[16,16,1024]{2,1,0:T(8,128)(2,1)}, u32[]{:S(2)}) copy-start(bf16[16,16,1024]{2,1,0:T(8,128)(2,1)} %copy-done.6) | copy-start | bytes 1572868
  98.1 60.2 %all-to-all-start.1 = ((bf16[8,256,512]{2,1,0:T(8,128)(2,1)}), bf16[8,256,512]{2,1,0:T(8,128)(2,1)}, u32[]{:S(2)}, u32[]{:S(2)}) async-start(bf16[8,256,512]{2,1,0:T(8,128)(2,1)} %bitcast.135), calls=%async_computation.1 | async-start | bytes 4194304 | tf_op jit(solution)/shard_map/all_to_all | solution.py:18
  102.7 215.0 %reduce-scatter.3.cloned.1.call-start = ((), (), s32[]{:S(2)}) async-start(), calls=%async_computation.7 | async-start | bytes 8912896 | tf_op jit(solution)/shard_map/reduce_scatter | solution.py:78
  160.3 1.7 copy-start.8
  161.9 41.4 %all-to-all-start.2 = ((bf16[8,256,512]{1,2,0:T(8,128)(2,1)}), bf16[8,256,512]{1,2,0:T(8,128)(2,1)S(1)}, u32[]{:S(2)}, u32[]{:S(2)}) async-start(bf16[8,256,512]{1,2,0:T(8,128)(2,1)} %broadcast_in_dim.101), calls=%async_computation.3 | async-start | bytes 4194304 | tf_op jit(solution)/shard_map/all_to_all | solution.py:30
  166.8 233.7 %reduce-scatter.5.cloned.1.call-start = ((), (), s32[]{:S(2)}) async-start(), calls=%async_computation.10 | async-start | bytes 4456448 | tf_op jit(solution)/shard_map/reduce_scatter | solution.py:55
  186.6 16.7 %copy-start.9 = (f32[256,256]{0,1:T(8,128)S(1)}, f32[256,256]{0,1:T(8,128)}, u32[]{:S(2)}) copy-start(f32[256,256]{0,1:T(8,128)} %copy.86) | copy-start | bytes 786436
  203.4 3.1 copy-start.2
  203.4 3.2 copy-start.4
  262.5 3.9 copy-start.5
  271.7 1.6 copy-start.3
  275.4 45.3 %all-to-all-start.3 = ((bf16[16,256,256]{1,2,0:T(8,128)(2,1)}), bf16[16,256,256]{1,2,0:T(8,128)(2,1)}, u32[]{:S(2)}, u32[]{:S(2)}) async-start(bf16[16,256,256]{1,2,0:T(8,128)(2,1)} %bitcast.134), calls=%async_computation.4 | async-start | bytes 4194304 | tf_op jit(solution)/shard_map/all_to_all | solution.py:18
  317.7 84.5 %copy-start.1 = (bf16[256,4096]{1,0:T(8,128)(2,1)S(1)}, bf16[256,4096]{1,0:T(8,128)(2,1)}, u32[]{:S(2)}) copy-start(bf16[256,4096]{1,0:T(8,128)(2,1)} %param.19) | copy-start | bytes 6291460
Sparse Core Ops, SparseCore 0:
  10.5 80.3 all-gather.3
  93.9 55.5 all-gather.5
  151.8 51.5 all-gather.7
  207.5 110.1 reduce-scatter.2
  321.5 78.9 reduce-scatter.4
where the time goes:
time: 411 us; the launch traced here: 409 us
  waiting for transfers between devices  234 us (57%)
  matrix products  66 us (16%)
  local copies, waits for them, and re-layouts  54.2 us (13%)
  starting transfers between devices  21.3 us (5%)
  other arithmetic  18.1 us (4%)
  between operations  14.7 us (4%)
    reduce_scatter x1, waiting for transfers between devices, sent_together(): lax.psum_scatter(both, axis, scatter_dimension=dim, tiled=True)  77.2 us
    all_gather x1, waiting for transfers between devices, body(): lax.all_gather(w_proj, 'seq', axis=0, tiled=True)  49.9 us
    all_gather x1, waiting for transfers between devices, in_one_piece(): lax.all_gather(both, axis, axis=dim, tiled=True)  38.1 us
    reduce_scatter x1, waiting for transfers between devices, body(): lax.psum_scatter(lax.dot_general(y_in, natural, (((0,), (0,)), ((), ())),...  37.9 us
    dynamic_slice x24, local copies, waits for them, and re-layouts, body(): lax.scan(statistics, start_stats, (key_blocks, pos_blocks))  20.8 us
    dot_general x16, matrix products, scores_of(): jnp.einsum('qhd,khd->hqk', query_heads, key_block, preferred_element_type...  20.8 us
    all_to_all x1, waiting for transfers between devices, body(): lax.all_to_all(outgoing, 'seq', split_axis=0, concat_axis=0, tiled=True)  16.4 us
    all_gather x1, waiting for transfers between devices, body(): lax.all_gather(w_out, 'seq', axis=1, tiled=True)  12.7 us
  transfers between devices with their start and end apart: 9, of which 6 were waited for; matrix products, arithmetic and copies ran while one was open for 33% of the time, Pallas kernels for 0%

commit v1 on v0

v1 whole, which is shorter than its diff:
```python
import math

import jax
import jax.numpy as jnp
from jax import lax
from jax.experimental import pallas as pl
from jax.experimental.pallas import tpu as pltpu
from jax.sharding import Mesh
from jax.sharding import PartitionSpec as P

HEAD_DIM = 128
SIZE = {"y": 4, "xh": 2, "c": 2, "z": 4, "xl": 2}
SCALE = 1.0 / math.sqrt(HEAD_DIM)
flt = jnp.float32
half = jnp.bfloat16


def shift(x, axis, k):
    n = SIZE[axis]
    return lax.ppermute(x, axis, [(i, (i + k) % n) for i in range(n)])


def dyn(x, i, axis=0):
    return lax.dynamic_index_in_dim(x, i, axis, keepdims=False)


def dot(a, b, ca, cb):
    return lax.dot_general(a, b, (((ca,), (cb,)), ((), ())), preferred_element_type=flt)


def dot16(a, b, ca, cb):
    return dot(a, b, ca, cb).astype(half)


def added(*parts):
    total = parts[0].astype(flt)
    for p in parts[1:]:
        total = total + p.astype(flt)
    return total.astype(half)


def one_hot_rows(target, n):
    rows = lax.broadcasted_iota(jnp.int32, (n, target.shape[-1]), 0)
    return (rows == target[..., None, :]).astype(half)


def in_group(first, groups):
    return (first[..., :, None] * 16 + jnp.arange(16, dtype=jnp.int32)).reshape(
        *first.shape[:-1], groups * 16
    )


def nt(a, b):
    return lax.dot_general(a, b, (((1,), (1,)), ((), ())), preferred_element_type=flt)


def nn(a, b):
    return lax.dot_general(a, b, (((1,), (0,)), ((), ())), preferred_element_type=flt)


def tn(a, b):
    return lax.dot_general(a, b, (((0,), (0,)), ((), ())), preferred_element_type=flt)


def allowed_of(bk, bq, n):
    ik = lax.broadcasted_iota(jnp.int32, (n, n), 0)
    iq = lax.broadcasted_iota(jnp.int32, (n, n), 1)
    return (ik + bk * n) <= (iq + bq * n)


def scores(k, q):
    return nt(k, q) * SCALE


def stats_kernel(bq_ref, bk_ref, q_ref, k_ref, out_ref):
    for h in range(2):
        cols = slice(h * HEAD_DIM, (h + 1) * HEAD_DIM)
        for i in range(4):
            m, t = h * 4 + i, 8 + h * 4 + i
            out_ref[m : m + 1, :] = jnp.full((1, 256), -1e30, flt)
            out_ref[t : t + 1, :] = jnp.zeros((1, 256), flt)
            for j in range(4):

                @pl.when(bk_ref[j] <= bq_ref[i])
                def _():
                    s = scores(k_ref[j, :, cols], q_ref[i, :, cols])
                    s = jnp.where(allowed_of(bk_ref[j], bq_ref[i], 256), s, -1e30)
                    before = out_ref[m : m + 1, :]
                    high = jnp.maximum(before, jnp.max(s, axis=0, keepdims=True))
                    total = jnp.sum(jnp.exp(s - high), axis=0, keepdims=True)
                    out_ref[t : t + 1, :] = out_ref[t : t + 1, :] * jnp.exp(before - high) + total
                    out_ref[m : m + 1, :] = high


def backward_kernel(
    bq_ref, bk_ref, c_ref, q_ref, o_ref, mine_ref, other_ref, k_ref, v_ref, stats_ref,
    keep_ref, send_ref, dkv_ref, g_ref, lse_ref, dl_ref, aq, ak, av,
):
    c = c_ref[0]
    for x in range(2):
        g_ref[x * 2 + c] = mine_ref[x]
        g_ref[x * 2 + 1 - c] = other_ref[x]
    high = jnp.max(stats_ref[:, 0:8, :], axis=0)
    total = jnp.sum(stats_ref[:, 8:16, :] * jnp.exp(stats_ref[:, 0:8, :] - high), axis=0)
    lse_ref[...] = high + jnp.log(total)
    ones = jnp.ones((8, HEAD_DIM), flt)
    aq[...] = jnp.zeros_like(aq)
    ak[...] = jnp.zeros_like(ak)
    av[...] = jnp.zeros_like(av)
    for h in range(2):
        cols = slice(h * HEAD_DIM, (h + 1) * HEAD_DIM)
        for i in range(4):
            row = h * 4 + i
            prod = g_ref[i, :, cols].astype(flt) * o_ref[i, :, cols].astype(flt)
            dl_ref[row : row + 1, :] = lax.dot_general(
                ones, prod, (((1,), (1,)), ((), ())),
                precision=lax.Precision.HIGHEST, preferred_element_type=flt,
            )[0:1]
            for j in range(4):

                @pl.when(bk_ref[j] <= bq_ref[i])
                def _():
                    q = q_ref[i, :, cols]
                    g = g_ref[i, :, cols]
                    k = k_ref[j, :, cols]
                    v = v_ref[j, :, cols]
                    w = jnp.exp(scores(k, q) - lse_ref[row : row + 1, :])
                    w = jnp.where(allowed_of(bk_ref[j], bq_ref[i], 256), w, 0.0)
                    d = nt(v, g)
                    ds = (w * (d - dl_ref[row : row + 1, :]) * SCALE).astype(half)
                    av[j, :, cols] += nn(w.astype(half), g)
                    ak[j, :, cols] += nn(ds, q)
                    aq[i, :, cols] += tn(ds, k)

    for x in range(2):
        keep_ref[x] = aq[x * 2 + c].astype(half)
        send_ref[x] = aq[x * 2 + 1 - c].astype(half)
    dkv_ref[:, :, :256] = ak[...].astype(half)
    dkv_ref[:, :, 256:] = av[...].astype(half)


def natural_kernel(c_ref, at_ref, lo_ref, hi_ref, w_ref, nat_ref, keep_ref, send_ref, ws, part):
    for j in range(4):
        for b in range(2):
            ws[:, b * 512 + j * 128 : b * 512 + (j + 1) * 128] = w_ref[j, :, b * 128 : (b + 1) * 128]
    rows = lax.broadcasted_iota(jnp.int32, (512, 512), 0)
    for x in range(2):
        hot = jnp.where(rows == at_ref[x : x + 1, :], 1.0, 0.0).astype(half)
        for b, ref in ((0, lo_ref), (1, hi_ref)):
            full = jnp.concatenate([ref[z * 2 + x] for z in range(4)], axis=0)
            nat_ref[x * 512 : (x + 1) * 512, b * 512 : (b + 1) * 512] = nn(hot, full).astype(half)
        part[x] = nt(nat_ref[x * 512 : (x + 1) * 512, :], ws[...]).astype(half).reshape(2, 256, 256)
    c = c_ref[0]
    for x in range(2):
        keep_ref[x] = part[x, c]
        send_ref[x] = part[x, 1 - c]


def late_kernel(z_ref, nat_ref, o_ref, term_ref, piece_ref):
    at = pl.multiple_of(z_ref[0] * 128, 128)
    for i in range(4):
        for b in range(2):
            piece_ref[i, :, b * 128 : (b + 1) * 128] = nat_ref[
                i * 256 : (i + 1) * 256, pl.ds(at + b * 512, 128)
            ]
    o = o_ref[...].reshape(1024, 256)
    for b in range(2):
        t = tn(o, nat_ref[:, b * 512 : (b + 1) * 512]).astype(half)
        for j in range(4):
            term_ref[j, :, b * 128 : (b + 1) * 128] = t[:, j * 128 : (j + 1) * 128]


def sorted_kernel(z_ref, target_ref, y_ref, out_ref):
    rows = lax.broadcasted_iota(jnp.int32, (256, 256), 0)
    hot = jnp.where(rows == target_ref[...], 1.0, 0.0).astype(half)
    for n in range(4):
        cols = nn(hot, y_ref[:, n * 256 : (n + 1) * 256]).astype(half)
        for j in range(4):
            out_ref[j * 4 + n] = cols[j * 64 : (j + 1) * 64]


VMEM = pl.BlockSpec(memory_space=pltpu.VMEM)
SMEM = pl.BlockSpec(memory_space=pltpu.SMEM)


def third(n):
    return pl.BlockSpec((4, 256, 256), lambda i: (0, 0, n))


def cost(flops):
    return pl.CostEstimate(flops=flops, bytes_accessed=2**21, transcendentals=0)


def shaped(*shape, dtype=half):
    return jax.ShapeDtypeStruct(shape, dtype)


def stats_of(bq, bk, side, kvw):
    return pl.pallas_call(
        stats_kernel,
        grid=(1,),
        out_shape=shaped(16, 256, dtype=flt),
        in_specs=[SMEM, SMEM, third(0), third(0)],
        out_specs=VMEM,
        cost_estimate=cost(3 * 2**30),
    )(bq, bk, side, kvw)


def backward_of(bq, bk, c, side, mine, other, kvw, stats):
    block = (4, 256, 256)
    return pl.pallas_call(
        backward_kernel,
        grid=(1,),
        out_shape=[shaped(2, 256, 256), shaped(2, 256, 256), shaped(4, 256, 512)],
        in_specs=[SMEM] * 3 + [third(0), third(1), VMEM, VMEM, third(0), third(1), VMEM],
        out_specs=[VMEM] * 3,
        scratch_shapes=[pltpu.VMEM(block, half)]
        + [pltpu.VMEM((8, 256), flt)] * 2
        + [pltpu.VMEM(block, flt)] * 3,
        cost_estimate=cost(6 * 2**30),
    )(bq, bk, c, side, side, mine, other, kvw, kvw, stats)


def natural_of(c, at, lo, hi, kvw):
    return pl.pallas_call(
        natural_kernel,
        grid=(1,),
        out_shape=[shaped(1024, 1024), shaped(2, 256, 256), shaped(2, 256, 256)],
        in_specs=[SMEM, VMEM, VMEM, VMEM, third(2)],
        out_specs=[VMEM] * 3,
        scratch_shapes=[pltpu.VMEM((256, 1024), half), pltpu.VMEM((2, 2, 256, 256), half)],
        cost_estimate=cost(2 * 2**30),
    )(c, at, lo, hi, kvw)


def late_of(z, natural, side):
    return pl.pallas_call(
        late_kernel,
        grid=(1,),
        out_shape=[shaped(4, 256, 256)] * 2,
        in_specs=[SMEM, VMEM, third(1)],
        out_specs=[VMEM] * 2,
        cost_estimate=cost(2**30),
    )(z, natural, side)


def sorted_of(z, target, y_in):
    return pl.pallas_call(
        sorted_kernel,
        grid_spec=pltpu.PrefetchScalarGridSpec(
            num_scalar_prefetch=1,
            grid=(1,),
            in_specs=[
                pl.BlockSpec((1, 256), lambda i, z: (0, 0)),
                pl.BlockSpec((256, 1024), lambda i, z: (0, z[0])),
            ],
            out_specs=pl.BlockSpec((16, 64, 256), lambda i, z: (0, 0, 0)),
        ),
        out_shape=shaped(16, 64, 256),
        cost_estimate=cost(2**28),
    )(z, target, y_in)


def exchanged(x, axes):
    return lax.all_to_all(x, axes, 0, 0, tiled=True)


def spread(x, axes, n):
    return exchanged(jnp.broadcast_to(x[None], (n, *x.shape)), axes)


def summed(x):
    return x.astype(flt).sum(axis=0).astype(half)


def target_of(first):
    at = jnp.sum(
        jnp.where(first[:, None] == jnp.arange(16), jnp.arange(16)[:, None], 0), axis=0
    )
    return in_group(at.astype(jnp.int32), 16)[None]


def body(d_bytes, owner_groups, block_order, y_in, w_proj, w_out, queries, keys, values, attn_out):
    y, xh, c, z, xl = (lax.axis_index(a) for a in ("y", "xh", "c", "z", "xl"))
    q = xh * 2 + c
    s = y * 4 + q
    i4 = jnp.arange(4, dtype=jnp.int32)
    i16 = jnp.arange(16, dtype=jnp.int32)
    seq, near, head = ("y", "xh", "c"), ("xh", "c"), ("z", "xl")
    one = lambda t: t.reshape(1).astype(jnp.int32)

    mine = dyn(owner_groups, s) // 16
    place = ((mine // 2) % 2) * 8 + (mine // 4) * 2 + mine % 2
    own = dot16(one_hot_rows(in_group(place, 16), 256), d_bytes, 1, 0)
    r10 = shift(own, "xh", 1)
    w_lo = spread(w_proj[:128], "y", 4).reshape(512, 1024)
    r01 = shift(own, "c", 1)
    r11 = shift(r10, "c", 1)
    rows = jnp.concatenate([own, r01, r10, r11], axis=0)
    w_hi = spread(w_proj[128:], "y", 4).reshape(512, 1024)

    landing = jnp.sum(
        jnp.where(owner_groups[:, :, None] // 16 == i16, owner_groups[:, :, None] % 16, 0), axis=1
    )

    y_own = sorted_of(one(z), target_of(dyn(landing, s, 1)), y_in)
    y_own = exchanged(y_own, seq).reshape(64, 16, 256)
    a = jnp.arange(64, dtype=jnp.int32)
    shard = ((a // 2) % 4) * 4 + ((a // 8) % 2) * 2 + a % 2
    y_own = jnp.take(y_own, shard * 4 + (q ^ (a // 16)), axis=0).reshape(1024, 256)
    y_all = spread(y_own, "z", 4).reshape(4, 1024, 256)

    def reduced(w):
        part = dot16(rows, w, 1, 1).reshape(8, 128, 512)
        block = summed(exchanged(part, head))
        block = exchanged(block.reshape(4, 32, 512), "y").reshape(128, 512)
        return spread(block, head, 8).reshape(8, 128, 512)

    lo, hi = reduced(w_lo), reduced(w_hi)

    src = jnp.arange(32, dtype=jnp.int32)
    owner = ((src // 2) % 4) * 4 + (q ^ (src // 8))
    to_shard = y * 4 + jnp.arange(2, dtype=jnp.int32)[:, None] * 2 + (src % 2)[None, :]
    at = landing.reshape(-1)[owner[None, :] * 16 + to_shard] + (src % 2)[None, :] * 16

    side = spread(jnp.concatenate([queries, attn_out], axis=1), near, 4).reshape(4, 256, 512)
    kvw = spread(jnp.concatenate([keys, values, w_out], axis=1), "y", 4).reshape(4, 256, 768)

    bq = lax.dynamic_slice_in_dim(block_order, y * 4, 4)
    bk = dyn(block_order.reshape(4, 4), q, 1)
    stats = spread(stats_of(bq, bk, side, kvw), near, 4).reshape(4, 16, 256)

    natural, keep, send = natural_of(one(c), in_group(at, 32), lo, hi, kvw)
    grad = added(keep, shift(send, "c", 1))
    grad = added(grad, shift(grad, "xh", 1))
    keep, send, dkv = backward_of(
        bq, bk, one(c), side, grad, shift(grad, "c", 1), kvw, stats
    )
    dkv = summed(exchanged(dkv, "y"))
    dq = added(keep, shift(send, "c", 1))
    dq = added(dyn(dq, xh), shift(dyn(dq, 1 - xh), "xh", 1))

    term, piece = late_of(one(z), natural, side)
    piece = lax.dynamic_slice_in_dim(exchanged(piece, near), xl * 2, 2)
    layer_grad = piece.transpose(1, 0, 2).reshape(256, 512)
    grad_out = summed(exchanged(term, "y"))

    terms = lax.dot_general(
        y_all, rows, (((1,), (0,)), ((), ())), preferred_element_type=flt
    ).astype(half)
    grad_proj = summed(exchanged(terms, "y"))
    return layer_grad, grad_proj, grad_out, dq, dkv[:, :256], dkv[:, 256:]


def solution(mesh):
    axes = ("y", "xh", "c", "z", "xl")
    finer = Mesh(mesh.devices.reshape([SIZE[a] for a in axes]), axes)
    seq, head = ("y", "xh", "c"), ("z", "xl")
    both = P(seq, head)
    placed = (both, P(), P(), P(seq, None), both, P(head, seq), both, both, both, both)
    return jax.shard_map(
        body,
        mesh=finer,
        in_specs=placed,
        out_specs=(both, both, P(head, seq), both, both, both),
        check_vma=False,
    )
```

time: 411 us -> 321 us (0.78)
  waiting for transfers between devices: 234 us -> 154 us
  matrix products: 66 us -> 13.4 us
  starting transfers between devices: 21.3 us -> 69.8 us
  local copies, waits for them, and re-layouts: 54.2 us -> 22.2 us
  Pallas kernels: 0 us -> 25.2 us
  blocking collectives: 0 us -> 24 us
  between operations: 14.7 us -> 1.1 us
  other arithmetic: 18.1 us -> 10.1 us
    all_to_all x4 -> x15, waiting for transfers between devices: 16.4 us -> 145 us  [exchanged(): return lax.all_to_all(x, axes, 0, 0, tiled=True)]
    reduce_scatter x2 -> x0, waiting for transfers between devices: 115 us -> none  [the longest x1 77.2 us: sent_together(): lax.psum_scatter(both, axis, scatter_dimension=dim, tiled=True)]
    all_gather x3 -> x0, waiting for transfers between devices: 101 us -> none  [the longest x1 49.9 us: body(): lax.all_gather(w_proj, 'seq', axis=0, tiled=True)]
    dot_general x52 -> x4, matrix products: 66 us -> 13.4 us  [the longest x3 8.23 us: dot(): lax.dot_general(a, b, (((ca,), (cb,)), ((), ())), preferred_element_type=...]
    all_to_all x4 -> x15, starting transfers between devices: 21 us -> 64.9 us  [exchanged(): return lax.all_to_all(x, axes, 0, 0, tiled=True)]
    pallas_call x0 -> x5, Pallas kernels: none -> 25.2 us  [the longest x1 9.93 us: backward_of(): pl.pallas_call(backward_kernel, grid=(1,), out_shape=[shaped(2, 256, 256)...]
    all_to_all x0 -> x2, blocking collectives: none -> 24 us  [exchanged(): return lax.all_to_all(x, axes, 0, 0, tiled=True)]
    dynamic_slice x24 -> x3, local copies, waits for them, and re-layouts: 20.8 us -> 1.48 us  [the longest x2 0.9 us: dyn(): return lax.dynamic_index_in_dim(x, i, axis, keepdims=False)]
  transfers between devices with their start and end apart: 9 -> 23, of which waited for: 6 -> 17; matrix products, arithmetic and copies ran while one was open for 33% -> 10% of each run, Pallas kernels for 0% -> 7%
where the time goes in v1:
time: 321 us; the launch traced here: 319 us
  waiting for transfers between devices  154 us (48%)
  starting transfers between devices  69.8 us (22%)
  Pallas kernels  25.2 us (8%)
  blocking collectives  24 us (7%)
  local copies, waits for them, and re-layouts  22.2 us (7%)
  matrix products  13.4 us (4%)
  other arithmetic  10.1 us (3%)
    all_to_all x15, waiting for transfers between devices, exchanged(): return lax.all_to_all(x, axes, 0, 0, tiled=True)  145 us
    all_to_all x15, starting transfers between devices, exchanged(): return lax.all_to_all(x, axes, 0, 0, tiled=True)  64.9 us
    all_to_all x2, blocking collectives, exchanged(): return lax.all_to_all(x, axes, 0, 0, tiled=True)  24 us
    pallas_call x1, Pallas kernels, backward_of(): pl.pallas_call(backward_kernel, grid=(1,), out_shape=[shaped(2, 256, 256)...  9.93 us
    broadcast_in_dim x8, local copies, waits for them, and re-layouts, spread(): return exchanged(jnp.broadcast_to(x[None], (n, *x.shape)), axes)  9.02 us
    ppermute x8, waiting for transfers between devices, shift(): return lax.ppermute(x, axis, [(i, (i + k) % n) for i in range(n)])  8.99 us
    dot_general x3, matrix products, dot(): lax.dot_general(a, b, (((ca,), (cb,)), ((), ())), preferred_element_type=...  8.23 us
  transfers between devices with their start and end apart: 23, of which 17 were waited for; matrix products, arithmetic and copies ran while one was open for 10% of the time, Pallas kernels for 7%

profile of v1, /device:TPU:0, one launch (start us, length us, event | category | flops | bytes accessed | tf_op | source)
XLA Modules:
  0.0 319.3 jit_solution(8887054249900122834)
XLA Ops:
  0.7 0.8 add_select_fusion.1
  2.6 2.2 shard_map.147
  4.8 7.1 %all-to-all-start.11 = ((bf16[16,64,256]{2,1,0:T(8,128)(2,1)}), bf16[16,64,256]{2,1,0:T(8,128)(2,1)S(1)}, u32[]{:S(2)}, u32[]{:S(2)}) async-start(bf16[16,64,256]{2,1,0:T(8,128)(2,1)} %shard_map.147), calls=%async_computation.11 | async-start | bytes 1048576 | tf_op jit(solution)/shard_map/all_to_all | solution.py:265
  12.0 12.3 %all-to-all-done.11 = bf16[16,64,256]{2,1,0:T(8,128)(2,1)S(1)} async-done(((bf16[16,64,256]{2,1,0:T(8,128)(2,1)}), bf16[16,64,256]{2,1,0:T(8,128)(2,1)S(1)}, u32[]{:S(2)}, u32[]{:S(2)}) %all-to-all-start.11) | async-done | bytes 524320 | tf_op jit(solution)/shard_map/all_to_all | solution.py:265
  24.3 1.1 broadcast_in_dim.61
  25.4 3.5 %all-to-all-start.4 = ((bf16[4,128,1024]{2,1,0:T(8,128)(2,1)}), bf16[4,128,1024]{2,1,0:T(8,128)(2,1)S(1)}, u32[]{:S(2)}, u32[]{:S(2)}) async-start(bf16[4,128,1024]{2,1,0:T(8,128)(2,1)} %broadcast_in_dim.61), calls=%async_computation.4 | async-start | bytes 2097152 | tf_op jit(solution)/shard_map/all_to_all | solution.py:265
  29.0 14.7 %all-to-all-done.4 = bf16[4,128,1024]{2,1,0:T(8,128)(2,1)S(1)} async-done(((bf16[4,128,1024]{2,1,0:T(8,128)(2,1)}), bf16[4,128,1024]{2,1,0:T(8,128)(2,1)S(1)}, u32[]{:S(2)}, u32[]{:S(2)}) %all-to-all-start.4) | async-done | bytes 1048608 | tf_op jit(solution)/shard_map/all_to_all | solution.py:265
  43.7 1.2 broadcast_in_dim.65
  45.0 3.5 %all-to-all-start.9 = ((bf16[4,256,512]{2,1,0:T(8,128)(2,1)}), bf16[4,256,512]{2,1,0:T(8,128)(2,1)S(1)}, u32[]{:S(2)}, u32[]{:S(2)}) async-start(bf16[4,256,512]{2,1,0:T(8,128)(2,1)} %broadcast_in_dim.65), calls=%async_computation.9 | async-start | bytes 2097152 | tf_op jit(solution)/shard_map/all_to_all | solution.py:265
  48.6 15.8 %all-to-all-done.9.o_ref.q_ref = bf16[4,256,512]{2,1,0:T(8,128)(2,1)S(1)} async-done(((bf16[4,256,512]{2,1,0:T(8,128)(2,1)}), bf16[4,256,512]{2,1,0:T(8,128)(2,1)S(1)}, u32[]{:S(2)}, u32[]{:S(2)}) %all-to-all-start.9) | async-done | bytes 1048608 | tf_op jit(solution)/shard_map/all_to_all | solution.py:265
  64.4 1.3 broadcast_in_dim.64
  66.0 3.6 %all-to-all-start.8 = ((bf16[4,256,768]{2,1,0:T(8,128)(2,1)}), bf16[4,256,768]{2,1,0:T(8,128)(2,1)S(1)}, u32[]{:S(2)}, u32[]{:S(2)}) async-start(bf16[4,256,768]{2,1,0:T(8,128)(2,1)} %broadcast_in_dim.64), calls=%async_computation.8 | async-start | bytes 3145728 | tf_op jit(solution)/shard_map/all_to_all | solution.py:265
  69.5 0.7 fusion.40
  71.2 19.0 %all-to-all-done.8.w_ref.k_ref.v_ref = bf16[4,256,768]{2,1,0:T(8,128)(2,1)S(1)} async-done(((bf16[4,256,768]{2,1,0:T(8,128)(2,1)}), bf16[4,256,768]{2,1,0:T(8,128)(2,1)S(1)}, u32[]{:S(2)}, u32[]{:S(2)}) %all-to-all-start.8) | async-done | bytes 1572896 | tf_op jit(solution)/shard_map/all_to_all | solution.py:265
  90.2 1.2 broadcast_in_dim.58
  91.4 4.2 %all-to-all-start = ((bf16[4,128,1024]{2,1,0:T(8,128)(2,1)}), bf16[4,128,1024]{2,1,0:T(8,128)(2,1)}, u32[]{:S(2)}, u32[]{:S(2)}) async-start(bf16[4,128,1024]{2,1,0:T(8,128)(2,1)} %broadcast_in_dim.58), calls=%async_computation | async-start | bytes 2097152 | tf_op jit(solution)/shard_map/all_to_all | solution.py:265
  97.6 4.6 %shard_map.148 = f32[16,256]{1,0:T(8,128)} custom-call(s32[4]{0:T(128)} %dynamic_slice.28.bq_ref, s32[4]{0:T(128)} %dynamic-slice_reduce_fusion.1.bk_ref, bf16[4,256,512]{2,1,0:T(8,128)(2,1)} %copy-done.3, bf16[4,256,768]{2,1,0:T(8,128)(2,1)} %copy-done.1), custom_call_target="tpu_custom_call" | custom-call | flops 3221225472 | bytes 2097152 | tf_op jit(solution)/shard_map/pallas_call | solution.py:199
  102.2 7.7 %all-to-all-done = bf16[4,128,1024]{2,1,0:T(8,128)(2,1)} async-done(((bf16[4,128,1024]{2,1,0:T(8,128)(2,1)}), bf16[4,128,1024]{2,1,0:T(8,128)(2,1)}, u32[]{:S(2)}, u32[]{:S(2)}) %all-to-all-start) | async-done | bytes 1048608 | tf_op jit(solution)/shard_map/all_to_all | solution.py:265
  109.9 1.4 broadcast_in_dim.118
  111.3 3.3 %all-to-all-start.15 = ((f32[4,16,256]{2,1,0:T(8,128)}), f32[4,16,256]{2,1,0:T(8,128)S(1)}, u32[]{:S(2)}, u32[]{:S(2)}) async-start(f32[4,16,256]{2,1,0:T(8,128)} %broadcast_in_dim.118), calls=%async_computation.15 | async-start | bytes 131072 | tf_op jit(solution)/shard_map/all_to_all | solution.py:265
  114.6 4.0 %convolution_convert_fusion = bf16[1024,512]{1,0:T(8,128)(2,1)} fusion(bf16[512,1024]{1,0:T(8,128)(2,1)} %bitcast.41, bf16[256,1024]{1,0:T(8,128)(2,1)} %collective-permute-done.2, bf16[256,1024]{1,0:T(8,128)(2,1)} %collective-permute-done.1, bf16[256,1024]{1,0:T(8,128)(2,1)} %collective-permute-done, bf16[256,1024]{1,0:T(8,128)(2,1)S(1)} %convolution_convert_fusion.2), kind=kOutput, calls=%fused_computation.6 | convolution fusion | flops 1082654720 | bytes 4194304 | tf_op jit(solution)/shard_map/dot_general | solution.py:28
  118.6 1.6 all-to-all-done.15.stats_ref
  120.2 5.3 %all-to-all-start.5 = ((bf16[8,128,512]{2,1,0:T(8,128)(2,1)}), bf16[8,128,512]{2,1,0:T(8,128)(2,1)S(1)}, u32[]{:S(2)}, u32[]{:S(2)}) async-start(bf16[8,128,512]{2,1,0:T(8,128)(2,1)} %bitcast.8), calls=%async_computation.5 | async-start | bytes 2097152 | tf_op jit(solution)/shard_map/all_to_all | solution.py:265
  125.5 3.9 %convolution_convert_fusion.1 = bf16[1024,512]{1,0:T(8,128)(2,1)} fusion(bf16[512,1024]{1,0:T(8,128)(2,1)} %bitcast.3, bf16[256,1024]{1,0:T(8,128)(2,1)} %collective-permute-done.2, bf16[256,1024]{1,0:T(8,128)(2,1)} %collective-permute-done.1, bf16[256,1024]{1,0:T(8,128)(2,1)} %collective-permute-done, bf16[256,1024]{1,0:T(8,128)(2,1)S(1)} %convolution_convert_fusion.2), kind=kOutput, calls=%fused_computation.7 | convolution fusion | flops 1082654720 | bytes 4194304 | tf_op jit(solution)/shard_map/dot_general | solution.py:28
  129.5 11.6 %all-to-all-done.5 = bf16[8,128,512]{2,1,0:T(8,128)(2,1)S(1)} async-done(((bf16[8,128,512]{2,1,0:T(8,128)(2,1)}), bf16[8,128,512]{2,1,0:T(8,128)(2,1)S(1)}, u32[]{:S(2)}, u32[]{:S(2)}) %all-to-all-start.5) | async-done | bytes 1048608 | tf_op jit(solution)/shard_map/all_to_all | solution.py:265
  141.0 3.6 %all-to-all-start.1 = ((bf16[8,128,512]{2,1,0:T(8,128)(2,1)}), bf16[8,128,512]{2,1,0:T(8,128)(2,1)S(1)}, u32[]{:S(2)}, u32[]{:S(2)}) async-start(bf16[8,128,512]{2,1,0:T(8,128)(2,1)} %bitcast.42), calls=%async_computation.1 | async-start | bytes 2097152 | tf_op jit(solution)/shard_map/all_to_all | solution.py:265
  144.6 0.8 reduce_sum.80
  145.4 14.1 %all-to-all-done.1 = bf16[8,128,512]{2,1,0:T(8,128)(2,1)S(1)} async-done(((bf16[8,128,512]{2,1,0:T(8,128)(2,1)}), bf16[8,128,512]{2,1,0:T(8,128)(2,1)S(1)}, u32[]{:S(2)}, u32[]{:S(2)}) %all-to-all-start.1) | async-done | bytes 1048608 | tf_op jit(solution)/shard_map/all_to_all | solution.py:265
  159.6 3.3 %all-to-all-start.6 = ((bf16[4,32,512]{2,1,0:T(8,128)(2,1)}), bf16[4,32,512]{2,1,0:T(8,128)(2,1)S(1)}, u32[]{:S(2)}, u32[]{:S(2)}) async-start(bf16[4,32,512]{2,1,0:T(8,128)(2,1)} %bitcast.9), calls=%async_computation.6 | async-start | bytes 262144 | tf_op jit(solution)/shard_map/all_to_all | solution.py:265
  163.0 5.8 %all-to-all-done.6 = bf16[4,32,512]{2,1,0:T(8,128)(2,1)S(1)} async-done(((bf16[4,32,512]{2,1,0:T(8,128)(2,1)}), bf16[4,32,512]{2,1,0:T(8,128)(2,1)S(1)}, u32[]{:S(2)}, u32[]{:S(2)}) %all-to-all-start.6) | async-done | bytes 131104 | tf_op jit(solution)/shard_map/all_to_all | solution.py:265
  168.8 8.3 %all_to_all.85 = bf16[4,32,512]{2,1,0:T(8,128)(2,1)S(1)} all-to-all(bf16[4,32,512]{2,1,0:T(8,128)(2,1)S(1)} %bitcast.45), channel_id=1, replica_groups=mesh['y'=4,'xh'=2,'c'=2,'z'=4,'xl'=2] {'y'}, dimensions={0} | all-to-all | bytes 262144 | tf_op jit(solution)/shard_map/all_to_all | solution.py:265
  177.3 15.6 %all_to_all.86.hi_ref = bf16[8,128,512]{2,1,0:T(8,128)(2,1)} all-to-all(bf16[8,128,512]{2,1,0:T(8,128)(2,1)S(1)} %broadcast_in_dim.63), channel_id=1, replica_groups=mesh['y'=4,'xh'=2,'c'=2,'z'=4,'xl'=2] {'z','xl'}, dimensions={0} | all-to-all | bytes 2097152 | tf_op jit(solution)/shard_map/all_to_all | solution.py:265
  192.9 1.1 broadcast_in_dim.60
  194.0 3.6 %all-to-all-start.3 = ((bf16[8,128,512]{2,1,0:T(8,128)(2,1)}), bf16[8,128,512]{2,1,0:T(8,128)(2,1)S(1)}, u32[]{:S(2)}, u32[]{:S(2)}) async-start(bf16[8,128,512]{2,1,0:T(8,128)(2,1)} %broadcast_in_dim.60), calls=%async_computation.3 | async-start | bytes 2097152 | tf_op jit(solution)/shard_map/all_to_all | solution.py:265
  198.7 11.1 %all-to-all-done.3.lo_ref = bf16[8,128,512]{2,1,0:T(8,128)(2,1)S(1)} async-done(((bf16[8,128,512]{2,1,0:T(8,128)(2,1)}), bf16[8,128,512]{2,1,0:T(8,128)(2,1)S(1)}, u32[]{:S(2)}, u32[]{:S(2)}) %all-to-all-start.3) | async-done | bytes 1048608 | tf_op jit(solution)/shard_map/all_to_all | solution.py:265
  209.8 1.7 broadcast_in_dim.117
  211.4 3.8 %all-to-all-start.12 = ((bf16[4,1024,256]{1,2,0:T(8,128)(2,1)}), bf16[4,1024,256]{1,2,0:T(8,128)(2,1)S(1)}, u32[]{:S(2)}, u32[]{:S(2)}) async-start(bf16[4,1024,256]{1,2,0:T(8,128)(2,1)} %broadcast_in_dim.117), calls=%async_computation.12 | async-start | bytes 4194304 | tf_op jit(solution)/shard_map/all_to_all | solution.py:265
  215.5 0.8 gather_fusion
  217.3 5.0 %shard_map.145 = (bf16[1024,1024]{1,0:T(8,128)(2,1)}, bf16[2,256,256]{2,1,0:T(8,128)(2,1)}, bf16[2,256,256]{2,1,0:T(8,128)(2,1)}) custom-call(s32[1]{0:T(128)} %bitcast.1.c_ref, s32[2,512]{1,0:T(2,128)} %broadcast_add_fusion.at_ref, bf16[8,128,512]{2,1,0:T(8,128)(2,1)} %copy-done.5, bf16[8,128,512]{2,1,0:T(8,128)(2,1)} %all_to_all.86.hi_ref, ...), custom_call_target="tpu_custom_call" | custom-call | flops 2147483648 | bytes 2097152 | tf_op jit(solution)/shard_map/pallas_call | solution.py:225
  222.3 3.4 %shard_map.146 = (bf16[4,256,256]{2,1,0:T(8,128)(2,1)}, bf16[4,256,256]{2,1,0:T(8,128)(2,1)}) custom-call(s32[1]{0:T(128)} %bitcast.z_ref, bf16[1024,1024]{1,0:T(8,128)(2,1)} %get-tuple-element.14.nat_ref, bf16[4,256,512]{2,1,0:T(8,128)(2,1)} %copy-done.3), custom_call_target="tpu_custom_call" | custom-call | flops 1073741824 | bytes 2097152 | tf_op jit(solution)/shard_map/pallas_call | solution.py:237
  225.7 9.8 %all-to-all-done.12 = bf16[4,1024,256]{1,2,0:T(8,128)(2,1)S(1)} async-done(((bf16[4,1024,256]{1,2,0:T(8,128)(2,1)}), bf16[4,1024,256]{1,2,0:T(8,128)(2,1)S(1)}, u32[]{:S(2)}, u32[]{:S(2)}) %all-to-all-start.12) | async-done | bytes 2097184 | tf_op jit(solution)/shard_map/all_to_all | solution.py:265
  235.6 4.6 %all-to-all-start.10 = ((bf16[4,256,256]{2,1,0:T(8,128)(2,1)}), bf16[4,256,256]{2,1,0:T(8,128)(2,1)S(1)}, u32[]{:S(2)}, u32[]{:S(2)}) async-start(bf16[4,256,256]{2,1,0:T(8,128)(2,1)} %get-tuple-element.15), calls=%async_computation.10 | async-start | bytes 1048576 | tf_op jit(solution)/shard_map/all_to_all | solution.py:265
  240.7 9.8 %all-to-all-done.10 = bf16[4,256,256]{2,1,0:T(8,128)(2,1)S(1)} async-done(((bf16[4,256,256]{2,1,0:T(8,128)(2,1)}), bf16[4,256,256]{2,1,0:T(8,128)(2,1)S(1)}, u32[]{:S(2)}, u32[]{:S(2)}) %all-to-all-start.10) | async-done | bytes 524320 | tf_op jit(solution)/shard_map/all_to_all | solution.py:265
  250.5 0.8 copy-done.2
  251.3 3.5 %all-to-all-start.14 = ((bf16[4,256,256]{2,1,0:T(8,128)(2,1)}), bf16[4,256,256]{2,1,0:T(8,128)(2,1)S(1)}, u32[]{:S(2)}, u32[]{:S(2)}) async-start(bf16[4,256,256]{2,1,0:T(8,128)(2,1)} %get-tuple-element.16), calls=%async_computation.14 | async-start | bytes 1048576 | tf_op jit(solution)/shard_map/all_to_all | solution.py:265
  254.8 5.2 %fusion.2 = bf16[4,256,1024]{2,1,0:T(8,128)(2,1)} fusion(bf16[4,1024,256]{1,2,0:T(8,128)(2,1)S(1)} %all-to-all-done.12, bf16[256,1024]{1,0:T(8,128)(2,1)} %collective-permute-done.2, bf16[256,1024]{1,0:T(8,128)(2,1)} %collective-permute-done.1, bf16[256,1024]{1,0:T(8,128)(2,1)} %collective-permute-done, bf16[256,1024]{1,0:T(8,128)(2,1)} %copy-done.6), kind=kOutput, calls=%fused_computation.5 | convolution fusion | flops 2156920832 | bytes 6291456 | tf_op jit(solution)/shard_map/dot_general | solution.py:348
  260.0 4.2 %all-to-all-done.14 = bf16[4,256,256]{2,1,0:T(8,128)(2,1)S(1)} async-done(((bf16[4,256,256]{2,1,0:T(8,128)(2,1)}), bf16[4,256,256]{2,1,0:T(8,128)(2,1)S(1)}, u32[]{:S(2)}, u32[]{:S(2)}) %all-to-all-start.14) | async-done | bytes 524320 | tf_op jit(solution)/shard_map/all_to_all | solution.py:265
  264.2 3.6 %all-to-all-start.13 = ((bf16[4,256,1024]{2,1,0:T(8,128)(2,1)}), bf16[4,256,1024]{2,1,0:T(8,128)(2,1)S(1)}, u32[]{:S(2)}, u32[]{:S(2)}) async-start(bf16[4,256,1024]{2,1,0:T(8,128)(2,1)} %fusion.2), calls=%async_computation.13 | async-start | bytes 4194304 | tf_op jit(solution)/shard_map/all_to_all | solution.py:265
  267.8 1.0 add_convert_fusion.2
  268.9 0.9 collective-permute-start.4
  269.7 7.3 %collective-permute-done.4 = bf16[2,256,256]{2,1,0:T(8,128)(2,1)S(1)} collective-permute-done((bf16[2,256,256]{2,1,0:T(8,128)(2,1)S(1)}, bf16[2,256,256]{2,1,0:T(8,128)(2,1)S(1)}, u32[]{:S(2)}, u32[]{:S(2)}) %collective-permute-start.4) | collective-permute-done | bytes 262176 | tf_op jit(solution)/shard_map/ppermute | solution.py:20
  277.2 1.7 collective-permute-done.5.other_ref
  278.9 9.9 %shard_map.149 = (bf16[2,256,256]{2,1,0:T(8,128)(2,1)}, bf16[2,256,256]{2,1,0:T(8,128)(2,1)}, bf16[4,256,512]{2,1,0:T(8,128)(2,1)}) custom-call(s32[4]{0:T(128)} %dynamic_slice.28.bq_ref, s32[4]{0:T(128)} %dynamic-slice_reduce_fusion.1.bk_ref, s32[1]{0:T(128)} %bitcast.1.c_ref, bf16[4,256,512]{2,1,0:T(8,128)(2,1)} %copy-done.3, ...), custom_call_target="tpu_custom_call" | custom-call | flops 6442450944 | bytes 2097152 | tf_op jit(solution)/shard_map/pallas_call | solution.py:211
  288.8 4.1 %all-to-all-done.13 = bf16[4,256,1024]{2,1,0:T(8,128)(2,1)S(1)} async-done(((bf16[4,256,1024]{2,1,0:T(8,128)(2,1)}), bf16[4,256,1024]{2,1,0:T(8,128)(2,1)S(1)}, u32[]{:S(2)}, u32[]{:S(2)}) %all-to-all-start.13) | async-done | bytes 2097184 | tf_op jit(solution)/shard_map/all_to_all | solution.py:265
  292.9 8.3 %all-to-all-start.16 = ((bf16[4,256,512]{2,1,0:T(8,128)(2,1)}), bf16[4,256,512]{2,1,0:T(8,128)(2,1)}, u32[]{:S(2)}, u32[]{:S(2)}) async-start(bf16[4,256,512]{2,1,0:T(8,128)(2,1)} %get-tuple-element.21), calls=%async_computation.16 | async-start | bytes 2097152 | tf_op jit(solution)/shard_map/all_to_all | solution.py:265
  302.0 1.1 add_convert_fusion
  303.8 2.5 collective-permute-start.7
  306.2 1.7 dynamic-slice_bitcast_fusion
  307.9 1.8 copy.24
  309.7 1.8 copy.26
  311.5 0.7 reduce_sum.83
  312.2 1.3 reduce_sum.82
  314.2 2.9 all-to-all-done.16
  317.1 1.5 reduce_sum.84
  (90 shorter events, 10.5 us)
Async XLA Ops:
  0.6 69.8 %copy-start = (bf16[256,1024]{1,0:T(8,128)(2,1)S(1)}, bf16[256,1024]{1,0:T(8,128)(2,1)}, u32[]{:S(2)}) copy-start(bf16[256,1024]{1,0:T(8,128)(2,1)} %param.10) | copy-start | bytes 1572868
  0.6 11.3 %copy-start.7 = (bf16[256,1024]{1,0:T(8,128)(2,1)S(1)}, bf16[256,1024]{1,0:T(8,128)(2,1)}, u32[]{:S(2)}) copy-start(bf16[256,1024]{1,0:T(8,128)(2,1)} %param.14) | copy-start | bytes 1572868
  4.8 19.5 %all-to-all-start.11 = ((bf16[16,64,256]{2,1,0:T(8,128)(2,1)}), bf16[16,64,256]{2,1,0:T(8,128)(2,1)S(1)}, u32[]{:S(2)}, u32[]{:S(2)}) async-start(bf16[16,64,256]{2,1,0:T(8,128)(2,1)} %shard_map.147), calls=%async_computation.11 | async-start | bytes 1048576 | tf_op jit(solution)/shard_map/all_to_all | solution.py:265
  12.0 17.0 %copy-start.11 = (bf16[256,256]{1,0:T(8,128)(2,1)S(1)}, bf16[256,256]{1,0:T(8,128)(2,1)}, u32[]{:S(2)}) copy-start(bf16[256,256]{1,0:T(8,128)(2,1)} %param.19) | copy-start | bytes 393220
  12.0 17.0 %copy-start.12 = (bf16[256,256]{1,0:T(8,128)(2,1)S(1)}, bf16[256,256]{1,0:T(8,128)(2,1)}, u32[]{:S(2)}) copy-start(bf16[256,256]{1,0:T(8,128)(2,1)} %param.16) | copy-start | bytes 393220
  25.4 18.3 %all-to-all-start.4 = ((bf16[4,128,1024]{2,1,0:T(8,128)(2,1)}), bf16[4,128,1024]{2,1,0:T(8,128)(2,1)S(1)}, u32[]{:S(2)}, u32[]{:S(2)}) async-start(bf16[4,128,1024]{2,1,0:T(8,128)(2,1)} %broadcast_in_dim.61), calls=%async_computation.4 | async-start | bytes 2097152 | tf_op jit(solution)/shard_map/all_to_all | solution.py:265
  28.9 19.6 %copy-start.13 = (bf16[256,256]{1,0:T(8,128)(2,1)S(1)}, bf16[256,256]{1,0:T(8,128)(2,1)}, u32[]{:S(2)}) copy-start(bf16[256,256]{1,0:T(8,128)(2,1)} %param.15) | copy-start | bytes 393220
  28.9 19.6 %copy-start.14 = (bf16[256,256]{1,0:T(8,128)(2,1)S(1)}, bf16[256,256]{1,0:T(8,128)(2,1)}, u32[]{:S(2)}) copy-start(bf16[256,256]{1,0:T(8,128)(2,1)} %param.18) | copy-start | bytes 393220
  28.9 19.6 %copy-start.15 = (bf16[256,256]{1,0:T(8,128)(2,1)S(1)}, bf16[256,256]{1,0:T(8,128)(2,1)}, u32[]{:S(2)}) copy-start(bf16[256,256]{1,0:T(8,128)(2,1)} %param.17) | copy-start | bytes 393220
  43.7 1.3 copy-start.4
  45.0 19.4 %all-to-all-start.9 = ((bf16[4,256,512]{2,1,0:T(8,128)(2,1)}), bf16[4,256,512]{2,1,0:T(8,128)(2,1)S(1)}, u32[]{:S(2)}, u32[]{:S(2)}) async-start(bf16[4,256,512]{2,1,0:T(8,128)(2,1)} %broadcast_in_dim.65), calls=%async_computation.9 | async-start | bytes 2097152 | tf_op jit(solution)/shard_map/all_to_all | solution.py:265
  64.4 1.5 copy-start.3
  66.0 24.2 %all-to-all-start.8 = ((bf16[4,256,768]{2,1,0:T(8,128)(2,1)}), bf16[4,256,768]{2,1,0:T(8,128)(2,1)S(1)}, u32[]{:S(2)}, u32[]{:S(2)}) async-start(bf16[4,256,768]{2,1,0:T(8,128)(2,1)} %broadcast_in_dim.64), calls=%async_computation.8 | async-start | bytes 3145728 | tf_op jit(solution)/shard_map/all_to_all | solution.py:265
  70.4 25.9 %copy-start.17 = (s32[16]{0:T(128)S(1)}, s32[16]{0:T(128)}, u32[]{:S(2)}) copy-start(s32[16]{0:T(128)} %param.12) | copy-start | bytes 196
  70.7 54.8 %copy-start.6 = (bf16[256,1024]{1,0:T(8,128)(2,1)}, bf16[256,1024]{1,0:T(8,128)(2,1)S(1)}, u32[]{:S(2)}) copy-start(bf16[256,1024]{1,0:T(8,128)(2,1)S(1)} %convolution_convert_fusion.2) | copy-start | bytes 1572868
  70.7 25.0 %collective-permute-start.1 = (bf16[256,1024]{1,0:T(8,128)(2,1)S(1)}, bf16[256,1024]{1,0:T(8,128)(2,1)}, u32[]{:S(2)}, u32[]{:S(2)}) collective-permute-start(bf16[256,1024]{1,0:T(8,128)(2,1)S(1)} %convolution_convert_fusion.2), channel_id=1, source_target_pairs={{0,16},{16,0},{1,17},{17,1},{2,18},{18,2},{3,19},{19,3},{4,20},{20... | collective-permute-start | bytes 1572872 | tf_op jit(solution)/shard_map/ppermute | solution.py:20
  90.2 7.5 %copy-start.1 = (bf16[4,256,768]{2,1,0:T(8,128)(2,1)}, bf16[4,256,768]{2,1,0:T(8,128)(2,1)S(1)}, u32[]{:S(2)}) copy-start(bf16[4,256,768]{2,1,0:T(8,128)(2,1)S(1)} %all-to-all-done.8.w_ref.k_ref.v_ref) | copy-start | bytes 4718596
  91.4 18.5 %all-to-all-start = ((bf16[4,128,1024]{2,1,0:T(8,128)(2,1)}), bf16[4,128,1024]{2,1,0:T(8,128)(2,1)}, u32[]{:S(2)}, u32[]{:S(2)}) async-start(bf16[4,128,1024]{2,1,0:T(8,128)(2,1)} %broadcast_in_dim.58), calls=%async_computation | async-start | bytes 2097152 | tf_op jit(solution)/shard_map/all_to_all | solution.py:265
  95.7 18.9 %collective-permute-start = (bf16[256,1024]{1,0:T(8,128)(2,1)S(1)}, bf16[256,1024]{1,0:T(8,128)(2,1)}, u32[]{:S(2)}, u32[]{:S(2)}) collective-permute-start(bf16[256,1024]{1,0:T(8,128)(2,1)S(1)} %convolution_convert_fusion.2), channel_id=1, source_target_pairs={{0,8},{8,0},{1,9},{9,1},{2,10},{10,2},{3,11},{11,3},{4,12},{12,4},... | collective-permute-start | bytes 1572872 | tf_op jit(solution)/shard_map/ppermute | solution.py:20
  95.8 18.8 %collective-permute-start.2 = (bf16[256,1024]{1,0:T(8,128)(2,1)}, bf16[256,1024]{1,0:T(8,128)(2,1)}, u32[]{:S(2)}, u32[]{:S(2)}) collective-permute-start(bf16[256,1024]{1,0:T(8,128)(2,1)} %collective-permute-done.1), channel_id=1, source_target_pairs={{0,8},{8,0},{1,9},{9,1},{2,10},{10,2},{3,11},{11,3},{4,12},{12,4},... | collective-permute-start | bytes 1572872 | tf_op jit(solution)/shard_map/ppermute | solution.py:20
  111.3 8.9 %all-to-all-start.15 = ((f32[4,16,256]{2,1,0:T(8,128)}), f32[4,16,256]{2,1,0:T(8,128)S(1)}, u32[]{:S(2)}, u32[]{:S(2)}) async-start(f32[4,16,256]{2,1,0:T(8,128)} %broadcast_in_dim.118), calls=%async_computation.15 | async-start | bytes 131072 | tf_op jit(solution)/shard_map/all_to_all | solution.py:265
  120.2 9.3 %copy-start.16 = (f32[4,16,256]{2,1,0:T(8,128)}, f32[4,16,256]{2,1,0:T(8,128)S(1)}, u32[]{:S(2)}) copy-start(f32[4,16,256]{2,1,0:T(8,128)S(1)} %all-to-all-done.15.stats_ref) | copy-start | bytes 196612
  120.2 20.9 %all-to-all-start.5 = ((bf16[8,128,512]{2,1,0:T(8,128)(2,1)}), bf16[8,128,512]{2,1,0:T(8,128)(2,1)S(1)}, u32[]{:S(2)}, u32[]{:S(2)}) async-start(bf16[8,128,512]{2,1,0:T(8,128)(2,1)} %bitcast.8), calls=%async_computation.5 | async-start | bytes 2097152 | tf_op jit(solution)/shard_map/all_to_all | solution.py:265
  141.0 18.5 %all-to-all-start.1 = ((bf16[8,128,512]{2,1,0:T(8,128)(2,1)}), bf16[8,128,512]{2,1,0:T(8,128)(2,1)S(1)}, u32[]{:S(2)}, u32[]{:S(2)}) async-start(bf16[8,128,512]{2,1,0:T(8,128)(2,1)} %bitcast.42), calls=%async_computation.1 | async-start | bytes 2097152 | tf_op jit(solution)/shard_map/all_to_all | solution.py:265
  159.6 9.3 %all-to-all-start.6 = ((bf16[4,32,512]{2,1,0:T(8,128)(2,1)}), bf16[4,32,512]{2,1,0:T(8,128)(2,1)S(1)}, u32[]{:S(2)}, u32[]{:S(2)}) async-start(bf16[4,32,512]{2,1,0:T(8,128)(2,1)} %bitcast.9), calls=%async_computation.6 | async-start | bytes 262144 | tf_op jit(solution)/shard_map/all_to_all | solution.py:265
  194.0 15.8 %all-to-all-start.3 = ((bf16[8,128,512]{2,1,0:T(8,128)(2,1)}), bf16[8,128,512]{2,1,0:T(8,128)(2,1)S(1)}, u32[]{:S(2)}, u32[]{:S(2)}) async-start(bf16[8,128,512]{2,1,0:T(8,128)(2,1)} %broadcast_in_dim.60), calls=%async_computation.3 | async-start | bytes 2097152 | tf_op jit(solution)/shard_map/all_to_all | solution.py:265
  209.8 1.7 copy-start.5
  211.4 24.1 %all-to-all-start.12 = ((bf16[4,1024,256]{1,2,0:T(8,128)(2,1)}), bf16[4,1024,256]{1,2,0:T(8,128)(2,1)S(1)}, u32[]{:S(2)}, u32[]{:S(2)}) async-start(bf16[4,1024,256]{1,2,0:T(8,128)(2,1)} %broadcast_in_dim.117), calls=%async_computation.12 | async-start | bytes 4194304 | tf_op jit(solution)/shard_map/all_to_all | solution.py:265
  235.6 14.9 %all-to-all-start.10 = ((bf16[4,256,256]{2,1,0:T(8,128)(2,1)}), bf16[4,256,256]{2,1,0:T(8,128)(2,1)S(1)}, u32[]{:S(2)}, u32[]{:S(2)}) async-start(bf16[4,256,256]{2,1,0:T(8,128)(2,1)} %get-tuple-element.15), calls=%async_computation.10 | async-start | bytes 1048576 | tf_op jit(solution)/shard_map/all_to_all | solution.py:265
  240.2 27.6 %collective-permute-start.3 = (bf16[2,256,256]{2,1,0:T(8,128)(2,1)}, bf16[2,256,256]{2,1,0:T(8,128)(2,1)}, u32[]{:S(2)}, u32[]{:S(2)}) collective-permute-start(bf16[2,256,256]{2,1,0:T(8,128)(2,1)} %get-tuple-element.18), channel_id=1, source_target_pairs={{0,8},{8,0},{1,9},{9,1},{2,10},{10,2},{3,11},{11,3},{4,12},{12,4},... | collective-permute-start | bytes 786440 | tf_op jit(solution)/shard_map/ppermute | solution.py:20
  250.5 0.8 copy-start.2
  251.3 12.9 %all-to-all-start.14 = ((bf16[4,256,256]{2,1,0:T(8,128)(2,1)}), bf16[4,256,256]{2,1,0:T(8,128)(2,1)S(1)}, u32[]{:S(2)}, u32[]{:S(2)}) async-start(bf16[4,256,256]{2,1,0:T(8,128)(2,1)} %get-tuple-element.16), calls=%async_computation.14 | async-start | bytes 1048576 | tf_op jit(solution)/shard_map/all_to_all | solution.py:265
  260.0 7.9 %copy-start.8 = (bf16[2,256,256]{2,1,0:T(8,128)(2,1)S(1)}, bf16[2,256,256]{2,1,0:T(8,128)(2,1)}, u32[]{:S(2)}) copy-start(bf16[2,256,256]{2,1,0:T(8,128)(2,1)} %get-tuple-element.17) | copy-start | bytes 786436
  264.2 28.7 %all-to-all-start.13 = ((bf16[4,256,1024]{2,1,0:T(8,128)(2,1)}), bf16[4,256,1024]{2,1,0:T(8,128)(2,1)S(1)}, u32[]{:S(2)}, u32[]{:S(2)}) async-start(bf16[4,256,1024]{2,1,0:T(8,128)(2,1)} %fusion.2), calls=%async_computation.13 | async-start | bytes 4194304 | tf_op jit(solution)/shard_map/all_to_all | solution.py:265
  268.9 8.2 %collective-permute-start.4 = (bf16[2,256,256]{2,1,0:T(8,128)(2,1)S(1)}, bf16[2,256,256]{2,1,0:T(8,128)(2,1)S(1)}, u32[]{:S(2)}, u32[]{:S(2)}) collective-permute-start(bf16[2,256,256]{2,1,0:T(8,128)(2,1)S(1)} %add_convert_fusion.2), channel_id=1, source_target_pairs={{0,16},{16,0},{1,17},{17,1},{2,18},{18,2},{3,19},{19,3},{4,20},{20... | collective-permute-start | bytes 786440 | tf_op jit(solution)/shard_map/ppermute | solution.py:20
  277.1 1.8 copy-start.10
  277.1 1.7 collective-permute-start.5
  288.8 12.5 %collective-permute-start.6 = (bf16[2,256,256]{2,1,0:T(8,128)(2,1)}, bf16[2,256,256]{2,1,0:T(8,128)(2,1)S(1)}, u32[]{:S(2)}, u32[]{:S(2)}) collective-permute-start(bf16[2,256,256]{2,1,0:T(8,128)(2,1)} %get-tuple-element.20), channel_id=1, source_target_pairs={{0,8},{8,0},{1,9},{9,1},{2,10},{10,2},{3,11},{11,3},{4,12},{12,4},... | collective-permute-start | bytes 786440 | tf_op jit(solution)/shard_map/ppermute | solution.py:20
  292.9 24.2 %all-to-all-start.16 = ((bf16[4,256,512]{2,1,0:T(8,128)(2,1)}), bf16[4,256,512]{2,1,0:T(8,128)(2,1)}, u32[]{:S(2)}, u32[]{:S(2)}) async-start(bf16[4,256,512]{2,1,0:T(8,128)(2,1)} %get-tuple-element.21), calls=%async_computation.16 | async-start | bytes 2097152 | tf_op jit(solution)/shard_map/all_to_all | solution.py:265
  301.3 0.7 copy-start.9
  303.8 9.8 %collective-permute-start.7 = (bf16[256,256]{1,0:T(8,128)(2,1)}, bf16[256,256]{1,0:T(8,128)(2,1)S(1)}, u32[]{:S(2)}, u32[]{:S(2)}) collective-permute-start(bf16[256,256]{1,0:T(8,128)(2,1)} %dynamic-slice_bitcast_fusion.1), channel_id=1, source_target_pairs={{0,16},{16,0},{1,17},{17,1},{2,18},{18,2},{3,19},{19,3},{4,20},{20... | collective-permute-start | bytes 393224 | tf_op jit(solution)/shard_map/ppermute | solution.py:20
